TPU v7x, 256 devices: a whole 4x4x8 slice. The times are simulated.
256 devices in a mesh: rep: 4 (over x), fsdp: 32 (over y, z), tp: 2 (over core).
Axes of the slice: x: 4, y: 4, z: 8, core: 2. Of those that a mesh axis runs over, the one named last changes fastest.
Arguments:
- saved_inputs: bfloat16 [2, 32768, 768], P(None, ('rep', 'fsdp')), may hold values from -24 to 24
- out_cotangent: float32 [32768, 768], P(('rep', 'fsdp')), may hold values from -1.75 to 1.75
- gate_weight: bfloat16 [2, 768, 4480], P(None, 'fsdp', 'tp'), may hold values from -0.21875 to 0.21875
- up_weight: bfloat16 [2, 768, 4480], P(None, 'fsdp', 'tp'), may hold values from -0.21875 to 0.21875
- down_weight: bfloat16 [2, 768, 4480], P(None, 'fsdp', 'tp'), may hold values from -0.09375 to 0.09375
- norm_gain: bfloat16 [2, 768], P(None, 'fsdp'), may hold values from 0.5 to 1.5
- gate_accum: float32 [2, 768, 4480], P(None, 'fsdp', 'tp'), may hold values from -12 to 12
- up_accum: float32 [2, 768, 4480], P(None, 'fsdp', 'tp'), may hold values from -12 to 12
- down_accum: float32 [2, 768, 4480], P(None, 'fsdp', 'tp'), may hold values from -12 to 12
- gain_accum: float32 [2, 768], P(None, 'fsdp'), may hold values from -12 to 12
Outputs:
- input_cotangent: float32 [32768, 768], P(('rep', 'fsdp'))
- gate_grad: float32 [2, 768, 4480], P(None, 'fsdp', 'tp')
- up_grad: float32 [2, 768, 4480], P(None, 'fsdp', 'tp')
- down_grad: float32 [2, 768, 4480], P(None, 'fsdp', 'tp')
- gain_grad: float32 [2, 768], P(None, 'fsdp')
All inputs are finite; a program needn't handle non-finite values.
Results may differ from a plain program's by a relative error of at most 0.0025.
Values may be sent and summed in bfloat16 or wider, within the bound.
No kernel may reach another device: no remote copies, remote signals or barrier semaphores. Data moves between devices by JAX's collectives and lax.ppermute only.
A program may use at most 192 MiB of HBM per device.

v0:
```python
import functools

import jax
import jax.numpy as jnp
from jax import lax
from jax.experimental import pallas as pl
from jax.experimental.pallas import tpu as pltpu
from jax.sharding import PartitionSpec as P

epsilon = 1e-06
F32, BF16, F16 = jnp.float32, jnp.bfloat16, jnp.float16


N_Y, N_Z, N_REP = 4, 8, 4
REP_STEPS = (1, 3, 2)
Y_STEPS = (1, 3, 2)
VMEM = pl.BlockSpec(memory_space=pltpu.VMEM)
SMEM = pl.BlockSpec(memory_space=pltpu.SMEM)


def shift_rep(value, step):
    return lax.ppermute(value, "rep", [(i, (i + step) % N_REP) for i in range(N_REP)])


def swap_tp(value):
    return lax.ppermute(value, "tp", [(0, 1), (1, 0)])


def shift_y(value, step):
    pairs = [(y * N_Z + z, (y + step) % N_Y * N_Z + z) for y in range(N_Y) for z in range(N_Z)]
    return lax.ppermute(value, "fsdp", pairs)


Y_GROUPS = [[y * N_Z + z for y in range(N_Y)] for z in range(N_Z)]
Z_GROUPS = [[y * N_Z + z for z in range(N_Z)] for y in range(N_Y)]


def exchange(value, axis, groups=None):
    return lax.all_to_all(value, axis, 0, 0, tiled=True, axis_index_groups=groups)


def after(value, *others):
    return lax.optimization_barrier((value, others))[0]


def pack_kernel(q, block, r_ref, gate_ref, up_ref, down_ref, gain_ref, *outs):
    for l, out in enumerate(outs):
        out[...] = jnp.zeros_like(out)
        out[:, q : q + 1] = gain_ref[l]
    for k in range(N_REP):

        @pl.when(r_ref[0] == k)
        def _():
            for l, out in enumerate(outs):
                for i, w in enumerate((gate_ref, up_ref, down_ref)):
                    out[:, i * block : i * block + q] = w[l, :, k * q : (k + 1) * q]


def pack(r, gate, up, down, gain, q, block):
    layers, rows, _ = gate.shape
    return pl.pallas_call(
        functools.partial(pack_kernel, q, block),
        out_shape=[jax.ShapeDtypeStruct((rows, 3 * block), BF16)] * layers,
        in_specs=[SMEM] + [VMEM] * 4,
        out_specs=[VMEM] * layers,
        cost_estimate=pl.CostEstimate(flops=1000000, bytes_accessed=1000000, transcendentals=0),
        name="pack",
    )(r.reshape(1), gate, up, down, gain[:, :, None])


def place_kernel(n, me_ref, *refs):
    out_ref = refs[n]
    for s in range(n):
        out_ref[lax.rem(me_ref[0] + (n - s), n)] = refs[s][...]


def place(me, pieces):
    n = len(pieces)
    return pl.pallas_call(
        functools.partial(place_kernel, n),
        out_shape=jax.ShapeDtypeStruct((n,) + pieces[0].shape, pieces[0].dtype),
        in_specs=[SMEM] + [VMEM] * n,
        out_specs=VMEM,
        cost_estimate=pl.CostEstimate(flops=1000000, bytes_accessed=2 * n * pieces[0].size * 2, transcendentals=0),
        name="place",
    )(me.reshape(1), *pieces)


def share_tokens(own, *others):
    moved = {s: shift_rep(own, s) for s in REP_STEPS}
    if others:
        moved = after(moved, *others)
    mine = jnp.stack([own] + [moved[s] for s in range(1, N_REP)])
    swapped = swap_tp(mine)
    return jnp.concatenate([mine, swapped], axis=0)


def products(block, normed_ref, u_ref, gg_ref, gu_ref, hid_ref, extra_ref, write):
    contract = (((0,), (0,)), ((), ()))
    for i, (left, right) in enumerate(((normed_ref, gg_ref), (normed_ref, gu_ref), (u_ref, hid_ref))):
        product = lax.dot_general(left[...], right[...], contract, preferred_element_type=F32)
        if i == 0:
            write(0, block - 128, product[:, : block - 128])
            write(block - 128, block, product[:, block - 128 :] + extra_ref[...])
        else:
            write(i * block, (i + 1) * block, product)


def grads_kernel(block, *refs):
    def write(start, stop, value):
        refs[6][:, start:stop] = value.astype(BF16)

    products(block, *refs[:6], write)


def grads_blocks_kernel(rows, block, y_ref, *refs):
    outs, acc = refs[6:10], refs[10]

    def write(start, stop, value):
        acc[:, : stop - start] = value
        for s in range(N_Y):
            first = pl.multiple_of(lax.rem(y_ref[0] + s, N_Y) * rows, rows)
            outs[s][:, start:stop] = acc[pl.ds(first, rows), : stop - start].astype(outs[s].dtype)

    products(block, *refs[:6], write)


def weight_grads(normed, u, gg, gu, hid, extra, y=None):
    tokens, d = normed.shape
    block = gg.shape[1]
    rows = d // N_Y
    if y is None:
        shapes, kernel, scratch, first = [(d, BF16)], functools.partial(grads_kernel, block), [], ()
    else:
        shapes, kernel = [(rows, F32)] + [(rows, BF16)] * 3, functools.partial(grads_blocks_kernel, rows, block)
        scratch, first = [pltpu.VMEM((d, block), F32)], (y.reshape(1),)
    return pl.pallas_call(
        kernel,
        out_shape=[jax.ShapeDtypeStruct((n, 3 * block), dtype) for n, dtype in shapes],
        in_specs=[SMEM] * len(first) + [VMEM] * 6,
        out_specs=[VMEM] * len(shapes),
        scratch_shapes=scratch,
        cost_estimate=pl.CostEstimate(flops=6 * tokens * d * block, bytes_accessed=10000000, transcendentals=0),
        compiler_params=pltpu.CompilerParams(vmem_limit_bytes=48 * 1024 * 1024),
        name="weight_grads",
    )(*first, normed, u, gg, gu, hid, extra)


def narrow(value, lane):
    most = jnp.max(jnp.abs(value), axis=-1, keepdims=True)
    e = jnp.where(most > 0.0, jnp.clip(jnp.ceil(jnp.log2(most)) - 12.0, -120.0, 120.0), 0.0)
    lanes = lax.broadcasted_iota(jnp.int32, value.shape, value.ndim - 1)
    return jnp.where(lanes == lane, e, value * jnp.exp2(-e)).astype(F16)


def widen(value, lane):
    return value.astype(F32) * jnp.exp2(value[..., lane : lane + 1].astype(F32))


def finish_kernel(q, block, layers, r_ref, b0, b1, b2, b3, *refs):
    accums, outs, stack = refs[:3], refs[3:6], refs[6]
    for s, b in enumerate((b0, b1, b2, b3)):
        stack[lax.rem(r_ref[0] + (N_REP - s), N_REP)] = b[...]
    for l in range(layers):
        for i in range(3):
            whole = jnp.concatenate([stack[k, l, :, i * block : i * block + q] for k in range(N_REP)], axis=1)
            outs[i][l] = accums[i][l] + whole


def finish(r, pieces, accums, q, block):
    return pl.pallas_call(
        functools.partial(finish_kernel, q, block, accums[0].shape[0]),
        out_shape=[jax.ShapeDtypeStruct(accums[0].shape, F32)] * 3,
        in_specs=[SMEM] + [VMEM] * 7,
        out_specs=[VMEM] * 3,
        scratch_shapes=[pltpu.VMEM((N_REP,) + pieces[0].shape, F32)],
        cost_estimate=pl.CostEstimate(flops=1000000, bytes_accessed=2000000, transcendentals=0),
        name="finish",
    )(r.reshape(1), *pieces, *accums)


def token_scale(x):
    x = x.astype(F32)
    return lax.rsqrt(jnp.mean(x * x, axis=1, keepdims=True) + epsilon)


def body(
    saved_inputs,
    out_cotangent,
    gate_weight,
    up_weight,
    down_weight,
    norm_gain,
    gate_accum,
    up_accum,
    down_accum,
    gain_accum,
):
    layers, tokens, d = saved_inputs.shape
    rows, hidden_local = gate_weight.shape[1:]
    q = hidden_local // N_REP
    block = -(-(q + 2) // 128) * 128
    half = tokens // 2
    r, f, t = lax.axis_index("rep"), lax.axis_index("fsdp"), lax.axis_index("tp")
    y = f // N_Z

    packed = pack(r, gate_weight, up_weight, down_weight, norm_gain, q, block)
    width = 3 * block
    top, low = layers - 1, 0

    line = exchange(jnp.broadcast_to(packed[top][None], (N_Z, rows, width)), "fsdp", Z_GROUPS)
    line = line.reshape(N_Z * rows, width)
    own_x = lax.dynamic_slice_in_dim(saved_inputs, t * half, half, 1)
    cotangent = lax.dynamic_slice_in_dim(out_cotangent, t * half, half, 0)
    shared = share_tokens(jnp.stack([own_x[top], cotangent.astype(BF16), own_x[low]]), line)
    moved = {s: shift_y(line, s) for s in Y_STEPS}
    x_top = shared[:, 0].reshape(8 * half, d)
    u_top = shared[:, 1].reshape(8 * half, d)
    scale_top = token_scale(x_top)
    moved = after(moved, u_top, scale_top)
    full_top = place(y, [line] + [moved[s] for s in range(1, N_Y)]).reshape(d, width)

    low_packed = after(packed[low], line)
    line = exchange(jnp.broadcast_to(low_packed[None], (N_Z, rows, width)), "fsdp", Z_GROUPS)
    line_low = line.reshape(N_Z * rows, width)
    cols = (((1,), (1,)), ((), ()))
    pick = (lax.broadcasted_iota(jnp.int32, (8, block), 1) == q).astype(BF16)

    def forward(x, u, w, scale):
        gate_w, up_w, down_w = w[:, :block], w[:, block : 2 * block], w[:, 2 * block :]
        gain = lax.dot_general(pick, gate_w, cols, preferred_element_type=F32)[0]
        white = x.astype(F32) * scale
        normed = (white * gain).astype(BF16)
        gate_pre = jnp.dot(normed, gate_w, preferred_element_type=F32)
        up_pre = jnp.dot(normed, up_w, preferred_element_type=F32)
        sig = jax.nn.sigmoid(gate_pre)
        active = gate_pre * sig
        hidden = (active * up_pre).astype(BF16)
        grad_hidden = jnp.dot(u, down_w, preferred_element_type=F32)
        grad_gate = (grad_hidden * up_pre * (sig * (1.0 + gate_pre * (1.0 - sig)))).astype(BF16)
        grad_up = (grad_hidden * active).astype(BF16)
        return gain, white, normed, hidden, grad_gate, grad_up

    def to_normed(grad_gate, grad_up, w):
        partial = lax.dot_general(grad_gate, w[:, :block], cols, preferred_element_type=F32)
        return partial + lax.dot_general(grad_up, w[:, block : 2 * block], cols, preferred_element_type=F32)

    def gain_columns(partial, white):
        gain_part = jnp.sum(partial * white, axis=0)
        gain_high = gain_part.astype(BF16).astype(F32)
        lane = lax.broadcasted_iota(jnp.int32, (d, 128), 1) - (q - block + 128)
        return jnp.where(lane == 0, gain_high[:, None], jnp.where(lane == 1, (gain_part - gain_high)[:, None], 0.0))

    def step_back(cotangent, own_x, grad_normed, gain):
        own = own_x.astype(F32)
        own_scale = lax.rsqrt(jnp.mean(own * own, axis=1, keepdims=True) + epsilon)
        own_white = own * own_scale
        grad_white = grad_normed * gain
        inner = jnp.mean(grad_white * own_white, axis=1, keepdims=True)
        return cotangent + own_scale * (grad_white - own_white * inner)

    gain, white, normed, hidden, gg, gu = forward(x_top, u_top, full_top, scale_top)
    partial = to_normed(gg, gu, full_top).reshape(8, half, d)
    mine = partial[:4] + swap_tp(partial[4:])
    moved = {s: shift_rep(mine[s], -s) for s in REP_STEPS}
    line_low = after(line_low, mine)
    moved_low = {s: shift_y(line_low, s) for s in Y_STEPS}
    extra = gain_columns(partial.reshape(8 * half, d), white)
    (grads_top,) = weight_grads(after(normed, mine, line_low), u_top, gg, gu, hidden, extra)
    received = exchange(grads_top.reshape(N_Y, N_Z * rows, width), "fsdp", Y_GROUPS)
    grad_normed = mine[0]
    for s in REP_STEPS:
        grad_normed = grad_normed + moved[s]
    cotangent = step_back(cotangent, own_x[top], grad_normed, gain)

    x_low = shared[:, 2].reshape(8 * half, d)
    u_low = share_tokens(cotangent.astype(BF16)).reshape(8 * half, d)
    moved_low, x_low = after((moved_low, x_low), cotangent, grads_top)
    full_low = place(y, [line_low] + [moved_low[s] for s in range(1, N_Y)]).reshape(d, width)
    gain, white, normed, hidden, gg, gu = forward(x_low, u_low, full_low, token_scale(x_low))
    partial = to_normed(gg, gu, full_low).reshape(8, half, d)
    extra = gain_columns(partial.reshape(8 * half, d), white)
    grads_low = weight_grads(normed, u_low, gg, gu, hidden, extra, y)
    moved_y = {s: shift_y(grads_low[s], s) for s in Y_STEPS}

    partial = after(partial, grads_low)
    mine = partial[:4] + swap_tp(partial[4:])
    moved = {s: shift_rep(mine[s], -s) for s in REP_STEPS}
    grad_normed = mine[0]
    for s in REP_STEPS:
        grad_normed = grad_normed + moved[s]
    cotangent = step_back(cotangent, own_x[low], grad_normed, gain)

    received = after(received, grads_low)
    total = jnp.sum(received.astype(F32), axis=0)
    shard_in = narrow(total, q + 2).reshape(N_Z, rows, width)
    shard_top = exchange(shard_in, "fsdp", Z_GROUPS)
    moved_y = after(moved_y, shard_in, mine)
    total = grads_low[0]
    for s in Y_STEPS:
        total = total + moved_y[s].astype(F32)
    shard_in = narrow(total, q + 2).reshape(N_Z, rows, width)
    shard_low = exchange(shard_in, "fsdp", Z_GROUPS)
    own = jnp.stack([narrow(jnp.sum(widen(v, q + 2), axis=0), q + 2) for v in (shard_low, shard_top)])
    moved = {s: shift_rep(own, s) for s in REP_STEPS}
    pieces = [widen(own, q + 2)] + [widen(moved[s], q + 2) for s in range(1, N_REP)]
    outs = finish(r, pieces, (gate_accum, up_accum, down_accum), q, block)
    gain_sum = sum(jnp.sum(b[:, :, q : q + 2], axis=2) for b in pieces)
    gain_grad = gain_accum + gain_sum + swap_tp(gain_sum)

    other = swap_tp(cotangent)
    both = jnp.stack([cotangent, other])
    cot_out = jnp.concatenate([lax.dynamic_index_in_dim(both, t, 0, False),
                               lax.dynamic_index_in_dim(both, 1 - t, 0, False)], axis=0)
    return (cot_out, outs[0], outs[1], outs[2], gain_grad)


def solution(mesh):
    return jax.shard_map(
        body,
        mesh=mesh,
        in_specs=(
            P(None, ("rep", "fsdp"), None),
            P(("rep", "fsdp"), None),
            P(None, "fsdp", "tp"),
            P(None, "fsdp", "tp"),
            P(None, "fsdp", "tp"),
            P(None, "fsdp"),
            P(None, "fsdp", "tp"),
            P(None, "fsdp", "tp"),
            P(None, "fsdp", "tp"),
            P(None, "fsdp"),
        ),
        out_specs=(
            P(("rep", "fsdp"), None),
            P(None, "fsdp", "tp"),
            P(None, "fsdp", "tp"),
            P(None, "fsdp", "tp"),
            P(None, "fsdp"),
        ),
        check_vma=False,
    )
```

profile of v0, /device:TPU:1, one launch (start us, length us, event | category | flops | bytes accessed | tf_op | source)
XLA Modules:
  0.0 345.6 jit_solution(2747542501689442301)
XLA Ops:
  2.1 1.9 pack.1
  4.0 1.8 broadcast_in_dim.93
  5.8 9.0 %all-to-all-start = ((bf16[8,24,1920]{2,1,0:T(8,128)(2,1)}), bf16[8,24,1920]{2,1,0:T(8,128)(2,1)S(1)}, u32[]{:S(2)}, u32[]{:S(2)}) async-start(bf16[8,24,1920]{2,1,0:T(8,128)(2,1)} %broadcast_in_dim.93), calls=%async_computation | async-start | bytes 1474560 | tf_op jit(solution)/shard_map/all_to_all | solution.py:39
  16.1 3.0 collective-permute-start.1
  19.4 2.4 collective-permute-start.2
  21.8 9.9 %collective-permute-done.1 = bf16[3,128,768]{2,1,0:T(8,128)(2,1)S(1)} collective-permute-done((bf16[3,128,768]{2,1,0:T(8,128)(2,1)S(1)}, bf16[3,128,768]{2,1,0:T(8,128)(2,1)S(1)}, u32[]{:S(2)}, u32[]{:S(2)}) %collective-permute-start.1) | collective-permute-done | bytes 589856 | tf_op jit(solution)/shard_map/ppermute | solution.py:22
  31.7 13.9 %collective-permute-done = bf16[3,128,768]{2,1,0:T(8,128)(2,1)S(1)} collective-permute-done((bf16[3,128,768]{2,1,0:T(8,128)(2,1)S(1)}, bf16[3,128,768]{2,1,0:T(8,128)(2,1)S(1)}, u32[]{:S(2)}, u32[]{:S(2)}) %collective-permute-start) | collective-permute-done | bytes 589856 | tf_op jit(solution)/shard_map/ppermute | solution.py:22
  46.5 3.1 pad_maximum_fusion
  50.1 2.8 collective-permute-start.6
  55.3 1.8 constant_dynamic-update-slice_fusion
  59.8 24.6 %collective-permute-done.6.refs_3_ = bf16[192,1920]{1,0:T(8,128)(2,1)S(1)} collective-permute-done((bf16[192,1920]{1,0:T(8,128)(2,1)S(1)}, bf16[192,1920]{1,0:T(8,128)(2,1)S(1)}, u32[]{:S(2)}, u32[]{:S(2)}) %collective-permute-start.6) | collective-permute-done | bytes 737312 | tf_op jit(solution)/shard_map/ppermute | solution.py:31
  84.4 4.2 %collective-permute-done.4.refs_1_ = bf16[192,1920]{1,0:T(8,128)(2,1)S(1)} collective-permute-done((bf16[192,1920]{1,0:T(8,128)(2,1)S(1)}, bf16[192,1920]{1,0:T(8,128)(2,1)S(1)}, u32[]{:S(2)}, u32[]{:S(2)}) %collective-permute-start.4) | collective-permute-done | bytes 737312 | tf_op jit(solution)/shard_map/ppermute | solution.py:31
  89.6 3.6 %place.2 = bf16[4,192,1920]{2,1,0:T(8,128)(2,1)} custom-call(s32[1]{0:T(128)} %bitcast.10.me_ref.y_ref, bf16[192,1920]{1,0:T(8,128)(2,1)} %bitcast.140, bf16[192,1920]{1,0:T(8,128)(2,1)} %copy-done.25, bf16[192,1920]{1,0:T(8,128)(2,1)} %copy-done.24, bf16[192,1920]{1,0:T(8,128)(2,1)} %copy-done.22), custom_call_target="tpu_custom_call" | custom-call | flops 1000000 | bytes 5898240 | tf_op jit(solution)/shard_map/place/pallas_call | solution.py:79
  93.2 2.7 fusion.9
  98.5 3.2 multiply_convert_fusion.4
  104.7 1.8 fusion.68
  107.9 6.6 %all-to-all-start.1 = ((bf16[8,24,1920]{2,1,0:T(8,128)(2,1)}), bf16[8,24,1920]{2,1,0:T(8,128)(2,1)}, u32[]{:S(2)}, u32[]{:S(2)}) async-start(bf16[8,24,1920]{2,1,0:T(8,128)(2,1)} %broadcast_in_dim.94), calls=%async_computation.1 | async-start | bytes 1474560 | tf_op jit(solution)/shard_map/all_to_all | solution.py:39
  114.6 2.1 add.163
  117.8 1.8 collective-permute-start.8
  121.3 15.9 %all-to-all-done.1 = bf16[8,24,1920]{2,1,0:T(8,128)(2,1)} async-done(((bf16[8,24,1920]{2,1,0:T(8,128)(2,1)}), bf16[8,24,1920]{2,1,0:T(8,128)(2,1)}, u32[]{:S(2)}, u32[]{:S(2)}) %all-to-all-start.1) | async-done | bytes 737312 | tf_op jit(solution)/shard_map/all_to_all | solution.py:39
  138.1 2.8 collective-permute-done.9
  142.5 2.1 constant_dynamic-update-slice_fusion.9
  147.0 6.9 %weight_grads.2 = bf16[768,1920]{1,0:T(8,128)(2,1)} custom-call(bf16[1024,768]{1,0:T(8,128)(2,1)S(1)} %multiply_convert_fusion.refs_0_, bf16[1024,768]{1,0:T(8,128)(2,1)} %bitcast.146, bf16[1024,640]{1,0:T(8,128)(2,1)S(1)} %copy-done.2, bf16[1024,640]{1,0:T(8,128)(2,1)S(1)} %get-tuple-element.81.refs_3_, bf16[1024,640]{1,0:T(8,128)(2,1)S(1)} %copy-done, ...), custom_call_target="tpu_custom_call" | custom-call | flops 3019898880 | bytes 10000000 | tf_op jit(solution)/shard_map/weight_grads/pallas_call | solution.py:137
  153.8 4.6 %all-to-all-start.2 = ((bf16[4,192,1920]{2,1,0:T(8,128)(2,1)}), bf16[4,192,1920]{2,1,0:T(8,128)(2,1)}, u32[]{:S(2)}, u32[]{:S(2)}) async-start(bf16[4,192,1920]{2,1,0:T(8,128)(2,1)} %bitcast.141), calls=%async_computation.2 | async-start | bytes 5898240 | tf_op jit(solution)/shard_map/all_to_all | solution.py:39
  159.9 2.2 pad_maximum_fusion.1
  162.1 2.3 collective-permute-start.14
  169.2 38.9 %collective-permute-done.15.refs_1_ = bf16[192,1920]{1,0:T(8,128)(2,1)S(1)} collective-permute-done((bf16[192,1920]{1,0:T(8,128)(2,1)}, bf16[192,1920]{1,0:T(8,128)(2,1)S(1)}, u32[]{:S(2)}, u32[]{:S(2)}) %collective-permute-start.15) | collective-permute-done | bytes 737312 | tf_op jit(solution)/shard_map/ppermute | solution.py:31
  209.0 3.6 %place.3 = bf16[4,192,1920]{2,1,0:T(8,128)(2,1)} custom-call(s32[1]{0:T(128)} %bitcast.10.me_ref.y_ref, bf16[192,1920]{1,0:T(8,128)(2,1)} %bitcast.27.refs_0_, bf16[192,1920]{1,0:T(8,128)(2,1)} %copy-done.23, bf16[192,1920]{1,0:T(8,128)(2,1)} %collective-permute-done.16.refs_2_, bf16[192,1920]{1,0:T(8,128)(2,1)} %collective-permute-done.17.refs_3_), custom_call_target="tpu_custom_call" | custom-call | flops 1000000 | bytes 5898240 | tf_op jit(solution)/shard_map/place/pallas_call | solution.py:79
  220.5 3.1 multiply_convert_fusion.1
  226.8 8.7 %weight_grads.3 = (f32[192,1920]{1,0:T(8,128)}, bf16[192,1920]{1,0:T(8,128)(2,1)S(1)}, bf16[192,1920]{1,0:T(8,128)(2,1)S(1)}, bf16[192,1920]{1,0:T(8,128)(2,1)S(1)}) custom-call(s32[1]{0:T(128)} %bitcast.10.me_ref.y_ref, bf16[1024,768]{1,0:T(8,128)(2,1)} %copy-done.19, bf16[1024,768]{1,0:T(8,128)(2,1)} %bitcast.150, ...), custom_call_target="tpu_custom_call" | custom-call | flops 3019898880 | bytes 10000000 | tf_op jit(solution)/shard_map/weight_grads/pallas_call | solution.py:137
  236.8 2.2 collective-permute-start.18
  239.2 1.8 collective-permute-start.24
  241.9 2.4 convert_reduce_fusion
  245.7 2.5 select_convert_fusion.1
  248.2 6.6 %all-to-all-start.4 = ((f16[8,24,1920]{2,1,0:T(8,128)(2,1)}), f16[8,24,1920]{2,1,0:T(8,128)(2,1)S(1)}, u32[]{:S(2)}, u32[]{:S(2)}) async-start(f16[8,24,1920]{2,1,0:T(8,128)(2,1)} %select_convert_fusion.1), calls=%async_computation.4 | async-start | bytes 1474560 | tf_op jit(solution)/shard_map/all_to_all | solution.py:39
  254.9 2.1 slice_add_fusion
  257.1 17.3 %collective-permute-done.23 = bf16[192,1920]{1,0:T(8,128)(2,1)} collective-permute-done((bf16[192,1920]{1,0:T(8,128)(2,1)S(1)}, bf16[192,1920]{1,0:T(8,128)(2,1)}, u32[]{:S(2)}, u32[]{:S(2)}) %collective-permute-start.23) | collective-permute-done | bytes 737312 | tf_op jit(solution)/shard_map/ppermute | solution.py:31
  274.7 1.8 collective-permute-start.19
  278.3 2.1 abs_reduce_fusion
  280.4 3.0 select_convert_fusion
  284.2 3.1 collective-permute-done.21
  287.3 10.2 %collective-permute-done.20 = f32[128,768]{1,0:T(8,128)S(1)} collective-permute-done((f32[128,768]{1,0:T(8,128)S(1)}, f32[128,768]{1,0:T(8,128)S(1)}, u32[]{:S(2)}, u32[]{:S(2)}) %collective-permute-start.20) | collective-permute-done | bytes 393248 | tf_op jit(solution)/shard_map/ppermute | solution.py:22
  297.7 6.7 %all-to-all-start.3 = ((f16[8,24,1920]{2,1,0:T(8,128)(2,1)}), f16[8,24,1920]{2,1,0:T(8,128)(2,1)S(1)}, u32[]{:S(2)}, u32[]{:S(2)}) async-start(f16[8,24,1920]{2,1,0:T(8,128)(2,1)} %bitcast.42), calls=%async_computation.3 | async-start | bytes 1474560 | tf_op jit(solution)/shard_map/all_to_all | solution.py:39
  307.9 19.0 %all-to-all-done.3 = f16[8,24,1920]{2,1,0:T(8,128)(2,1)S(1)} async-done(((f16[8,24,1920]{2,1,0:T(8,128)(2,1)}), f16[8,24,1920]{2,1,0:T(8,128)(2,1)S(1)}, u32[]{:S(2)}, u32[]{:S(2)}) %all-to-all-start.3) | async-done | bytes 737312 | tf_op jit(solution)/shard_map/all_to_all | solution.py:39
  328.0 2.7 collective-permute-start.28
  330.9 4.0 %collective-permute-done.26 = f16[2,24,1920]{2,1,0:T(8,128)(2,1)S(1)} collective-permute-done((f16[2,24,1920]{2,1,0:T(8,128)(2,1)S(1)}, f16[2,24,1920]{2,1,0:T(8,128)(2,1)S(1)}, u32[]{:S(2)}, u32[]{:S(2)}) %collective-permute-start.26) | collective-permute-done | bytes 184352 | tf_op jit(solution)/shard_map/ppermute | solution.py:22
  337.8 3.8 %collective-permute-start.29 = (f32[2,24]{1,0:T(2,128)S(1)}, f32[2,24]{1,0:T(2,128)S(1)}, u32[]{:S(2)}, u32[]{:S(2)}) collective-permute-start(f32[2,24]{1,0:T(2,128)S(1)} %add_add_fusion.1), channel_id=1, source_target_pairs={{0,1},{1,0},{2,3},{3,2},{4,5},{5,4},{6,7},{7,6},{8,9},{9,8},{10,11... | collective-permute-start | bytes 584 | tf_op jit(solution)/shard_map/ppermute | solution.py:26
  341.6 3.2 finish.1
  (183 shorter events, 58.5 us)
Async XLA Ops:
  0.6 14.1 %copy-start.26 = (bf16[2,256,768]{2,1,0:T(8,128)(2,1)S(1)}, bf16[2,256,768]{2,1,0:T(8,128)(2,1)}, u32[]{:S(2)}) copy-start(bf16[2,256,768]{2,1,0:T(8,128)(2,1)} %param.10) | copy-start | bytes 2359300
  5.8 40.7 %all-to-all-start = ((bf16[8,24,1920]{2,1,0:T(8,128)(2,1)}), bf16[8,24,1920]{2,1,0:T(8,128)(2,1)S(1)}, u32[]{:S(2)}, u32[]{:S(2)}) async-start(bf16[8,24,1920]{2,1,0:T(8,128)(2,1)} %broadcast_in_dim.93), calls=%async_computation | async-start | bytes 1474560 | tf_op jit(solution)/shard_map/all_to_all | solution.py:39
  14.9 35.1 %copy-start.12 = (bf16[1,128,768]{2,1,0:T(8,128)(2,1)}, bf16[1,128,768]{2,1,0:T(8,128)(2,1)S(1)}, u32[]{:S(2)}) copy-start(bf16[1,128,768]{2,1,0:T(8,128)(2,1)S(1)} %get-tuple-element.95) | copy-start | bytes 589828
  16.1 15.6 %collective-permute-start.1 = (bf16[3,128,768]{2,1,0:T(8,128)(2,1)S(1)}, bf16[3,128,768]{2,1,0:T(8,128)(2,1)S(1)}, u32[]{:S(2)}, u32[]{:S(2)}) collective-permute-start(bf16[3,128,768]{2,1,0:T(8,128)(2,1)S(1)} %get-tuple-element.97), channel_id=1, source_target_pairs={{0,128},{64,192},{128,0},{192,64},{1,129},{65,193},{129,1},{193,65... | collective-permute-start | bytes 1769480 | tf_op jit(solution)/shard_map/ppermute | solution.py:22
  19.1 26.5 %collective-permute-start = (bf16[3,128,768]{2,1,0:T(8,128)(2,1)S(1)}, bf16[3,128,768]{2,1,0:T(8,128)(2,1)S(1)}, u32[]{:S(2)}, u32[]{:S(2)}) collective-permute-start(bf16[3,128,768]{2,1,0:T(8,128)(2,1)S(1)} %get-tuple-element.97), channel_id=1, source_target_pairs={{0,64},{64,128},{128,192},{192,0},{1,65},{65,129},{129,193},{193,1... | collective-permute-start | bytes 1769480 | tf_op jit(solution)/shard_map/ppermute | solution.py:22
  19.4 27.0 %collective-permute-start.2 = (bf16[3,128,768]{2,1,0:T(8,128)(2,1)S(1)}, bf16[3,128,768]{2,1,0:T(8,128)(2,1)S(1)}, u32[]{:S(2)}, u32[]{:S(2)}) collective-permute-start(bf16[3,128,768]{2,1,0:T(8,128)(2,1)S(1)} %get-tuple-element.97), channel_id=1, source_target_pairs={{0,192},{64,0},{128,64},{192,128},{1,193},{65,1},{129,65},{193,129... | collective-permute-start | bytes 1769480 | tf_op jit(solution)/shard_map/ppermute | solution.py:22
  46.5 6.8 %copy-start.13 = (bf16[8,24,1920]{2,1,0:T(8,128)(2,1)}, bf16[8,24,1920]{2,1,0:T(8,128)(2,1)S(1)}, u32[]{:S(2)}) copy-start(bf16[8,24,1920]{2,1,0:T(8,128)(2,1)S(1)} %all-to-all-done) | copy-start | bytes 2211844
  49.5 5.8 %collective-permute-start.3 = (bf16[4,3,128,768]{3,2,1,0:T(8,128)(2,1)}, bf16[4,3,128,768]{3,2,1,0:T(8,128)(2,1)}, u32[]{:S(2)}, u32[]{:S(2)}) collective-permute-start(bf16[4,3,128,768]{3,2,1,0:T(8,128)(2,1)} %pad_maximum_fusion), channel_id=1, source_target_pairs={{0,1},{1,0},{2,3},{3,2},{4,5},{5,4},{6,7},{7,6},{8,9},{9,8},{10,11... | collective-permute-start | bytes 7077896 | tf_op jit(solution)/shard_map/ppermute | solution.py:26
  50.1 34.3 %collective-permute-start.6 = (bf16[192,1920]{1,0:T(8,128)(2,1)S(1)}, bf16[192,1920]{1,0:T(8,128)(2,1)S(1)}, u32[]{:S(2)}, u32[]{:S(2)}) collective-permute-start(bf16[192,1920]{1,0:T(8,128)(2,1)S(1)} %bitcast.137), channel_id=1, source_target_pairs={{0,48},{2,50},{4,52},{6,54},{8,56},{10,58},{12,60},{14,62},{16,0},... | collective-permute-start | bytes 2211848 | tf_op jit(solution)/shard_map/ppermute | solution.py:31
  52.9 31.5 %collective-permute-start.5 = (bf16[192,1920]{1,0:T(8,128)(2,1)S(1)}, bf16[192,1920]{1,0:T(8,128)(2,1)S(1)}, u32[]{:S(2)}, u32[]{:S(2)}) collective-permute-start(bf16[192,1920]{1,0:T(8,128)(2,1)S(1)} %bitcast.138), channel_id=1, source_target_pairs={{0,32},{2,34},{4,36},{6,38},{8,40},{10,42},{12,44},{14,46},{16,48}... | collective-permute-start | bytes 2211848 | tf_op jit(solution)/shard_map/ppermute | solution.py:31
  53.3 35.4 %collective-permute-start.4 = (bf16[192,1920]{1,0:T(8,128)(2,1)S(1)}, bf16[192,1920]{1,0:T(8,128)(2,1)S(1)}, u32[]{:S(2)}, u32[]{:S(2)}) collective-permute-start(bf16[192,1920]{1,0:T(8,128)(2,1)S(1)} %bitcast.139), channel_id=1, source_target_pairs={{0,16},{2,18},{4,20},{6,22},{8,24},{10,26},{12,28},{14,30},{16,32}... | collective-permute-start | bytes 2211848 | tf_op jit(solution)/shard_map/ppermute | solution.py:31
  59.8 33.3 %copy-start.21 = (bf16[8,1,128,768]{3,2,1,0:T(8,128)(2,1)}, bf16[8,1,128,768]{3,2,1,0:T(8,128)(2,1)S(1)}, u32[]{:S(2)}) copy-start(bf16[8,1,128,768]{3,2,1,0:T(8,128)(2,1)S(1)} %get-tuple-element.83) | copy-start | bytes 4718596
  106.5 8.1 %collective-permute-start.7 = (f32[4,128,768]{2,1,0:T(8,128)}, f32[4,128,768]{2,1,0:T(8,128)}, u32[]{:S(2)}, u32[]{:S(2)}) collective-permute-start(f32[4,128,768]{2,1,0:T(8,128)} %bitcast.15), channel_id=1, source_target_pairs={{0,1},{1,0},{2,3},{3,2},{4,5},{5,4},{6,7},{7,6},{8,9},{9,8},{10,11... | collective-permute-start | bytes 4718600 | tf_op jit(solution)/shard_map/ppermute | solution.py:26
  107.9 29.3 %all-to-all-start.1 = ((bf16[8,24,1920]{2,1,0:T(8,128)(2,1)}), bf16[8,24,1920]{2,1,0:T(8,128)(2,1)}, u32[]{:S(2)}, u32[]{:S(2)}) async-start(bf16[8,24,1920]{2,1,0:T(8,128)(2,1)} %broadcast_in_dim.94), calls=%async_computation.1 | async-start | bytes 1474560 | tf_op jit(solution)/shard_map/all_to_all | solution.py:39
  117.8 20.3 %collective-permute-start.8 = (f32[128,768]{1,0:T(8,128)}, f32[128,768]{1,0:T(8,128)}, u32[]{:S(2)}, u32[]{:S(2)}) collective-permute-start(f32[128,768]{1,0:T(8,128)} %get-tuple-element.89), channel_id=1, source_target_pairs={{0,192},{64,0},{128,64},{192,128},{1,193},{65,1},{129,65},{193,129... | collective-permute-start | bytes 1179656 | tf_op jit(solution)/shard_map/ppermute | solution.py:22
  119.6 18.5 %collective-permute-start.10 = (f32[128,768]{1,0:T(8,128)}, f32[128,768]{1,0:T(8,128)}, u32[]{:S(2)}, u32[]{:S(2)}) collective-permute-start(f32[128,768]{1,0:T(8,128)} %get-tuple-element.90), channel_id=1, source_target_pairs={{0,128},{64,192},{128,0},{192,64},{1,129},{65,193},{129,1},{193,65... | collective-permute-start | bytes 1179656 | tf_op jit(solution)/shard_map/ppermute | solution.py:22
  121.0 19.8 %collective-permute-start.9 = (f32[128,768]{1,0:T(8,128)}, f32[128,768]{1,0:T(8,128)}, u32[]{:S(2)}, u32[]{:S(2)}) collective-permute-start(f32[128,768]{1,0:T(8,128)} %get-tuple-element.91), channel_id=1, source_target_pairs={{0,64},{64,128},{128,192},{192,0},{1,65},{65,129},{129,193},{193,1... | collective-permute-start | bytes 1179656 | tf_op jit(solution)/shard_map/ppermute | solution.py:22
  137.2 9.7 %copy-start = (bf16[1024,640]{1,0:T(8,128)(2,1)S(1)}, bf16[1024,640]{1,0:T(8,128)(2,1)}, u32[]{:S(2)}) copy-start(bf16[1024,640]{1,0:T(8,128)(2,1)} %get-tuple-element.79.refs_4_) | copy-start | bytes 3932164
  137.2 9.7 %copy-start.2 = (bf16[1024,640]{1,0:T(8,128)(2,1)S(1)}, bf16[1024,640]{1,0:T(8,128)(2,1)}, u32[]{:S(2)}) copy-start(bf16[1024,640]{1,0:T(8,128)(2,1)} %copy-done.1) | copy-start | bytes 3932164
  137.2 32.0 %collective-permute-start.17 = (bf16[192,1920]{1,0:T(8,128)(2,1)}, bf16[192,1920]{1,0:T(8,128)(2,1)}, u32[]{:S(2)}, u32[]{:S(2)}) collective-permute-start(bf16[192,1920]{1,0:T(8,128)(2,1)} %bitcast.27.refs_0_), channel_id=1, source_target_pairs={{0,48},{2,50},{4,52},{6,54},{8,56},{10,58},{12,60},{14,62},{16,0},... | collective-permute-start | bytes 2211848 | tf_op jit(solution)/shard_map/ppermute | solution.py:31
  137.9 31.4 %collective-permute-start.16 = (bf16[192,1920]{1,0:T(8,128)(2,1)}, bf16[192,1920]{1,0:T(8,128)(2,1)}, u32[]{:S(2)}, u32[]{:S(2)}) collective-permute-start(bf16[192,1920]{1,0:T(8,128)(2,1)} %bitcast.27.refs_0_), channel_id=1, source_target_pairs={{0,32},{2,34},{4,36},{6,38},{8,40},{10,42},{12,44},{14,46},{16,48}... | collective-permute-start | bytes 2211848 | tf_op jit(solution)/shard_map/ppermute | solution.py:31
  144.7 13.8 %collective-permute-start.13 = (bf16[128,768]{1,0:T(8,128)(2,1)}, bf16[128,768]{1,0:T(8,128)(2,1)}, u32[]{:S(2)}, u32[]{:S(2)}) collective-permute-start(bf16[128,768]{1,0:T(8,128)(2,1)} %get-tuple-element.70), channel_id=1, source_target_pairs={{0,192},{64,0},{128,64},{192,128},{1,193},{65,1},{129,65},{193,129... | collective-permute-start | bytes 589832 | tf_op jit(solution)/shard_map/ppermute | solution.py:22
  144.7 15.2 %collective-permute-start.12 = (bf16[128,768]{1,0:T(8,128)(2,1)}, bf16[128,768]{1,0:T(8,128)(2,1)}, u32[]{:S(2)}, u32[]{:S(2)}) collective-permute-start(bf16[128,768]{1,0:T(8,128)(2,1)} %get-tuple-element.70), channel_id=1, source_target_pairs={{0,128},{64,192},{128,0},{192,64},{1,129},{65,193},{129,1},{193,65... | collective-permute-start | bytes 589832 | tf_op jit(solution)/shard_map/ppermute | solution.py:22
  146.1 13.8 %collective-permute-start.11 = (bf16[128,768]{1,0:T(8,128)(2,1)}, bf16[128,768]{1,0:T(8,128)(2,1)}, u32[]{:S(2)}, u32[]{:S(2)}) collective-permute-start(bf16[128,768]{1,0:T(8,128)(2,1)} %get-tuple-element.70), channel_id=1, source_target_pairs={{0,64},{64,128},{128,192},{192,0},{1,65},{65,129},{129,193},{193,1... | collective-permute-start | bytes 589832 | tf_op jit(solution)/shard_map/ppermute | solution.py:22
  153.8 88.0 %all-to-all-start.2 = ((bf16[4,192,1920]{2,1,0:T(8,128)(2,1)}), bf16[4,192,1920]{2,1,0:T(8,128)(2,1)}, u32[]{:S(2)}, u32[]{:S(2)}) async-start(bf16[4,192,1920]{2,1,0:T(8,128)(2,1)} %bitcast.141), calls=%async_computation.2 | async-start | bytes 5898240 | tf_op jit(solution)/shard_map/all_to_all | solution.py:39
  158.5 49.7 %copy-start.3 = (bf16[8,1,128,768]{3,2,1,0:T(8,128)(2,1)S(1)}, bf16[8,1,128,768]{3,2,1,0:T(8,128)(2,1)}, u32[]{:S(2)}) copy-start(bf16[8,1,128,768]{3,2,1,0:T(8,128)(2,1)} %get-tuple-element.82) | copy-start | bytes 4718596
  158.5 49.7 %collective-permute-start.15 = (bf16[192,1920]{1,0:T(8,128)(2,1)}, bf16[192,1920]{1,0:T(8,128)(2,1)S(1)}, u32[]{:S(2)}, u32[]{:S(2)}) collective-permute-start(bf16[192,1920]{1,0:T(8,128)(2,1)} %bitcast.27.refs_0_), channel_id=1, source_target_pairs={{0,16},{2,18},{4,20},{6,22},{8,24},{10,26},{12,28},{14,30},{16,32}... | collective-permute-start | bytes 2211848 | tf_op jit(solution)/shard_map/ppermute | solution.py:31
  162.1 54.1 %collective-permute-start.14 = (bf16[4,128,768]{2,1,0:T(8,128)(2,1)}, bf16[4,128,768]{2,1,0:T(8,128)(2,1)}, u32[]{:S(2)}, u32[]{:S(2)}) collective-permute-start(bf16[4,128,768]{2,1,0:T(8,128)(2,1)} %pad_maximum_fusion.1), channel_id=1, source_target_pairs={{0,1},{1,0},{2,3},{3,2},{4,5},{5,4},{6,7},{7,6},{8,9},{9,8},{10,11... | collective-permute-start | bytes 2359304 | tf_op jit(solution)/shard_map/ppermute | solution.py:26
  226.5 9.0 %copy-start.7 = (f32[1024,768]{1,0:T(8,128)}, f32[1024,768]{1,0:T(8,128)S(1)}, u32[]{:S(2)}) copy-start(f32[1024,768]{1,0:T(8,128)S(1)} %get-tuple-element.107) | copy-start | bytes 9437188
  236.8 18.1 %collective-permute-start.18 = (f32[4,128,768]{2,1,0:T(8,128)}, f32[4,128,768]{2,1,0:T(8,128)}, u32[]{:S(2)}, u32[]{:S(2)}) collective-permute-start(f32[4,128,768]{2,1,0:T(8,128)} %slice.139), channel_id=1, source_target_pairs={{0,1},{1,0},{2,3},{3,2},{4,5},{5,4},{6,7},{7,6},{8,9},{9,8},{10,11... | collective-permute-start | bytes 4718600 | tf_op jit(solution)/shard_map/ppermute | solution.py:26
  239.0 35.3 %collective-permute-start.23 = (bf16[192,1920]{1,0:T(8,128)(2,1)S(1)}, bf16[192,1920]{1,0:T(8,128)(2,1)}, u32[]{:S(2)}, u32[]{:S(2)}) collective-permute-start(bf16[192,1920]{1,0:T(8,128)(2,1)S(1)} %get-tuple-element.48), channel_id=1, source_target_pairs={{0,16},{2,18},{4,20},{6,22},{8,24},{10,26},{12,28},{14,30},{16,32}... | collective-permute-start | bytes 2211848 | tf_op jit(solution)/shard_map/ppermute | solution.py:31
  239.2 35.1 %collective-permute-start.24 = (bf16[192,1920]{1,0:T(8,128)(2,1)S(1)}, bf16[192,1920]{1,0:T(8,128)(2,1)}, u32[]{:S(2)}, u32[]{:S(2)}) collective-permute-start(bf16[192,1920]{1,0:T(8,128)(2,1)S(1)} %get-tuple-element.49), channel_id=1, source_target_pairs={{0,32},{2,34},{4,36},{6,38},{8,40},{10,42},{12,44},{14,46},{16,48}... | collective-permute-start | bytes 2211848 | tf_op jit(solution)/shard_map/ppermute | solution.py:31
  241.0 33.7 %collective-permute-start.25 = (bf16[192,1920]{1,0:T(8,128)(2,1)S(1)}, bf16[192,1920]{1,0:T(8,128)(2,1)}, u32[]{:S(2)}, u32[]{:S(2)}) collective-permute-start(bf16[192,1920]{1,0:T(8,128)(2,1)S(1)} %get-tuple-element.50), channel_id=1, source_target_pairs={{0,48},{2,50},{4,52},{6,54},{8,56},{10,58},{12,60},{14,62},{16,0},... | collective-permute-start | bytes 2211848 | tf_op jit(solution)/shard_map/ppermute | solution.py:31
  248.2 49.5 %all-to-all-start.4 = ((f16[8,24,1920]{2,1,0:T(8,128)(2,1)}), f16[8,24,1920]{2,1,0:T(8,128)(2,1)S(1)}, u32[]{:S(2)}, u32[]{:S(2)}) async-start(f16[8,24,1920]{2,1,0:T(8,128)(2,1)} %select_convert_fusion.1), calls=%async_computation.4 | async-start | bytes 1474560 | tf_op jit(solution)/shard_map/all_to_all | solution.py:39
  257.0 21.3 %copy-start.11 = (f32[192,1920]{1,0:T(8,128)S(1)}, f32[192,1920]{1,0:T(8,128)}, u32[]{:S(2)}) copy-start(f32[192,1920]{1,0:T(8,128)} %get-tuple-element.47) | copy-start | bytes 4423684
  274.7 9.5 %collective-permute-start.19 = (f32[128,768]{1,0:T(8,128)S(1)}, f32[128,768]{1,0:T(8,128)S(1)}, u32[]{:S(2)}, u32[]{:S(2)}) collective-permute-start(f32[128,768]{1,0:T(8,128)S(1)} %get-tuple-element.86), channel_id=1, source_target_pairs={{0,192},{64,0},{128,64},{192,128},{1,193},{65,1},{129,65},{193,129... | collective-permute-start | bytes 1179656 | tf_op jit(solution)/shard_map/ppermute | solution.py:22
  276.5 10.8 %collective-permute-start.21 = (f32[128,768]{1,0:T(8,128)S(1)}, f32[128,768]{1,0:T(8,128)S(1)}, u32[]{:S(2)}, u32[]{:S(2)}) collective-permute-start(f32[128,768]{1,0:T(8,128)S(1)} %get-tuple-element.87), channel_id=1, source_target_pairs={{0,128},{64,192},{128,0},{192,64},{1,129},{65,193},{129,1},{193,65... | collective-permute-start | bytes 1179656 | tf_op jit(solution)/shard_map/ppermute | solution.py:22
  277.4 20.0 %collective-permute-start.20 = (f32[128,768]{1,0:T(8,128)S(1)}, f32[128,768]{1,0:T(8,128)S(1)}, u32[]{:S(2)}, u32[]{:S(2)}) collective-permute-start(f32[128,768]{1,0:T(8,128)S(1)} %get-tuple-element.88), channel_id=1, source_target_pairs={{0,64},{64,128},{128,192},{192,0},{1,65},{65,129},{129,193},{193,1... | collective-permute-start | bytes 1179656 | tf_op jit(solution)/shard_map/ppermute | solution.py:22
  283.3 21.0 %copy-start.20 = (f32[128,768]{1,0:T(8,128)S(1)}, f32[128,768]{1,0:T(8,128)}, u32[]{:S(2)}) copy-start(f32[128,768]{1,0:T(8,128)} %get-tuple-element.71) | copy-start | bytes 1179652
  297.7 29.2 %all-to-all-start.3 = ((f16[8,24,1920]{2,1,0:T(8,128)(2,1)}), f16[8,24,1920]{2,1,0:T(8,128)(2,1)S(1)}, u32[]{:S(2)}, u32[]{:S(2)}) async-start(f16[8,24,1920]{2,1,0:T(8,128)(2,1)} %bitcast.42), calls=%async_computation.3 | async-start | bytes 1474560 | tf_op jit(solution)/shard_map/all_to_all | solution.py:39
  304.6 2.2 collective-permute-start.22
  327.9 7.0 %collective-permute-start.26 = (f16[2,24,1920]{2,1,0:T(8,128)(2,1)S(1)}, f16[2,24,1920]{2,1,0:T(8,128)(2,1)S(1)}, u32[]{:S(2)}, u32[]{:S(2)}) collective-permute-start(f16[2,24,1920]{2,1,0:T(8,128)(2,1)S(1)} %pad_maximum_fusion.4), channel_id=1, source_target_pairs={{0,64},{64,128},{128,192},{192,0},{1,65},{65,129},{129,193},{193,1... | collective-permute-start | bytes 552968 | tf_op jit(solution)/shard_map/ppermute | solution.py:22
  328.0 7.2 %collective-permute-start.28 = (f16[2,24,1920]{2,1,0:T(8,128)(2,1)S(1)}, f16[2,24,1920]{2,1,0:T(8,128)(2,1)S(1)}, u32[]{:S(2)}, u32[]{:S(2)}) collective-permute-start(f16[2,24,1920]{2,1,0:T(8,128)(2,1)S(1)} %pad_maximum_fusion.4), channel_id=1, source_target_pairs={{0,192},{64,0},{128,64},{192,128},{1,193},{65,1},{129,65},{193,129... | collective-permute-start | bytes 552968 | tf_op jit(solution)/shard_map/ppermute | solution.py:22
  330.6 6.7 %collective-permute-start.27 = (f16[2,24,1920]{2,1,0:T(8,128)(2,1)S(1)}, f16[2,24,1920]{2,1,0:T(8,128)(2,1)S(1)}, u32[]{:S(2)}, u32[]{:S(2)}) collective-permute-start(f16[2,24,1920]{2,1,0:T(8,128)(2,1)S(1)} %pad_maximum_fusion.4), channel_id=1, source_target_pairs={{0,128},{64,192},{128,0},{192,64},{1,129},{65,193},{129,1},{193,65... | collective-permute-start | bytes 552968 | tf_op jit(solution)/shard_map/ppermute | solution.py:22
  330.7 10.9 %copy-start.15 = (f32[2,24,1920]{2,1,0:T(8,128)}, f32[2,24,1920]{2,1,0:T(8,128)S(1)}, u32[]{:S(2)}) copy-start(f32[2,24,1920]{2,1,0:T(8,128)S(1)} %convert_multiply_fusion.9.b0) | copy-start | bytes 1105924
  330.7 14.1 %copy-start.30 = (f32[2,24]{1,0:T(2,128)S(1)}, f32[2,24]{1,0:T(2,128)}, u32[]{:S(2)}) copy-start(f32[2,24]{1,0:T(2,128)} %param.19) | copy-start | bytes 580
  335.1 6.5 %copy-start.16 = (f32[2,24,1920]{2,1,0:T(8,128)}, f32[2,24,1920]{2,1,0:T(8,128)S(1)}, u32[]{:S(2)}) copy-start(f32[2,24,1920]{2,1,0:T(8,128)S(1)} %convert_multiply_fusion.8.b1) | copy-start | bytes 1105924
  337.8 7.0 %collective-permute-start.29 = (f32[2,24]{1,0:T(2,128)S(1)}, f32[2,24]{1,0:T(2,128)S(1)}, u32[]{:S(2)}, u32[]{:S(2)}) collective-permute-start(f32[2,24]{1,0:T(2,128)S(1)} %add_add_fusion.1), channel_id=1, source_target_pairs={{0,1},{1,0},{2,3},{3,2},{4,5},{5,4},{6,7},{7,6},{8,9},{9,8},{10,11... | collective-permute-start | bytes 584 | tf_op jit(solution)/shard_map/ppermute | solution.py:26
  (18 other events, 50.4 us)
where the time goes:
time: 351 us; the launch traced here: 346 us
  waiting for transfers between devices  167 us (48%)
  starting transfers between devices  70.2 us (20%)
  other arithmetic  31 us (9%)
  Pallas kernels  27.9 us (8%)
  local copies, waits for them, and re-layouts  26.5 us (8%)
  matrix products  21.2 us (6%)
    ppermute x9, waiting for transfers between devices, shift_y(): return lax.ppermute(value, 'fsdp', pairs)  85.3 us
    ppermute x15, waiting for transfers between devices, shift_rep(): lax.ppermute(value, 'rep', [(i, (i + step) % N_REP) for i in range(N_REP)])  46.3 us
    all_to_all x5, waiting for transfers between devices, exchange(): lax.all_to_all(value, axis, 0, 0, tiled=True, axis_index_groups=groups)  34.9 us
    all_to_all x5, starting transfers between devices, exchange(): lax.all_to_all(value, axis, 0, 0, tiled=True, axis_index_groups=groups)  33.6 us
    ppermute x15, starting transfers between devices, shift_rep(): lax.ppermute(value, 'rep', [(i, (i + step) % N_REP) for i in range(N_REP)])  17.5 us
    pallas_call x2, Pallas kernels, weight_grads(): pl.pallas_call(kernel, out_shape=[jax.ShapeDtypeStruct((n, 3 * block), dt...  15.6 us
    unnamed x68, local copies, waits for them, and re-layouts  12.1 us
    ppermute x6, starting transfers between devices, swap_tp(): return lax.ppermute(value, 'tp', [(0, 1), (1, 0)])  10.1 us
  transfers between devices with their start and end apart: 35, of which 16 were waited for; matrix products, arithmetic and copies ran while one was open for 15% of the time, Pallas kernels for 6%

commit v1 on v0

--- a/solution.py
+++ b/solution.py
@@ -43,29 +43,37 @@
     return lax.optimization_barrier((value, others))[0]
 
 
-def pack_kernel(q, block, r_ref, gate_ref, up_ref, down_ref, gain_ref, *outs):
+def pack_kernel(q, block, r_ref, gate_ref, up_ref, down_ref, gain_ref, *refs):
+    outs, one = refs[:-1], refs[-1]
+    rows = gate_ref.shape[1]
+    row = lax.broadcasted_iota(jnp.int32, (rows, rows), 0)
+    diagonal = row == lax.broadcasted_iota(jnp.int32, (rows, rows), 1)
     for l, out in enumerate(outs):
-        out[...] = jnp.zeros_like(out)
-        out[:, q : q + 1] = gain_ref[l]
-    for k in range(N_REP):
-
-        @pl.when(r_ref[0] == k)
-        def _():
-            for l, out in enumerate(outs):
+        gain = jnp.where(diagonal, gain_ref[l : l + 1].astype(F32), 0.0)
+        one[...] = jnp.zeros_like(one)
+        one[:, q : q + 1] = jnp.sum(gain, axis=1, keepdims=True).astype(BF16)
+        for k in range(N_REP):
+
+            @pl.when(r_ref[0] == k)
+            def _():
                 for i, w in enumerate((gate_ref, up_ref, down_ref)):
-                    out[:, i * block : i * block + q] = w[l, :, k * q : (k + 1) * q]
+                    one[:, i * block : i * block + q] = w[l, :, k * q : (k + 1) * q]
+
+        for i in range(N_Z):
+            out[i] = one[...]
 
 
 def pack(r, gate, up, down, gain, q, block):
     layers, rows, _ = gate.shape
     return pl.pallas_call(
         functools.partial(pack_kernel, q, block),
-        out_shape=[jax.ShapeDtypeStruct((rows, 3 * block), BF16)] * layers,
+        out_shape=[jax.ShapeDtypeStruct((N_Z, rows, 3 * block), BF16)] * layers,
         in_specs=[SMEM] + [VMEM] * 4,
         out_specs=[VMEM] * layers,
+        scratch_shapes=[pltpu.VMEM((rows, 3 * block), BF16)],
         cost_estimate=pl.CostEstimate(flops=1000000, bytes_accessed=1000000, transcendentals=0),
         name="pack",
-    )(r.reshape(1), gate, up, down, gain[:, :, None])
+    )(r.reshape(1), gate, up, down, gain)
 
 
 def place_kernel(n, me_ref, *refs):
@@ -208,7 +216,7 @@
     width = 3 * block
     top, low = layers - 1, 0
 
-    line = exchange(jnp.broadcast_to(packed[top][None], (N_Z, rows, width)), "fsdp", Z_GROUPS)
+    line = exchange(packed[top], "fsdp", Z_GROUPS)
     line = line.reshape(N_Z * rows, width)
     own_x = lax.dynamic_slice_in_dim(saved_inputs, t * half, half, 1)
     cotangent = lax.dynamic_slice_in_dim(out_cotangent, t * half, half, 0)
@@ -221,7 +229,7 @@
     full_top = place(y, [line] + [moved[s] for s in range(1, N_Y)]).reshape(d, width)
 
     low_packed = after(packed[low], line)
-    line = exchange(jnp.broadcast_to(low_packed[None], (N_Z, rows, width)), "fsdp", Z_GROUPS)
+    line = exchange(low_packed, "fsdp", Z_GROUPS)
     line_low = line.reshape(N_Z * rows, width)
     cols = (((1,), (1,)), ((), ()))
     pick = (lax.broadcasted_iota(jnp.int32, (8, block), 1) == q).astype(BF16)
@@ -264,9 +272,10 @@
     mine = partial[:4] + swap_tp(partial[4:])
     moved = {s: shift_rep(mine[s], -s) for s in REP_STEPS}
     line_low = after(line_low, mine)
-    moved_low = {s: shift_y(line_low, s) for s in Y_STEPS}
+    moved_low = {3: shift_y(line_low, 3)}
+    moved_low |= {s: shift_y(line_low, s) for s in (2, 1)}
     extra = gain_columns(partial.reshape(8 * half, d), white)
-    (grads_top,) = weight_grads(after(normed, mine, line_low), u_top, gg, gu, hidden, extra)
+    (grads_top,) = weight_grads(after(normed, mine), u_top, gg, gu, hidden, extra)
     received = exchange(grads_top.reshape(N_Y, N_Z * rows, width), "fsdp", Y_GROUPS)
     grad_normed = mine[0]
     for s in REP_STEPS:

time: 351 us -> 348 us (level)
  local copies, waits for them, and re-layouts: 26.5 us -> 22.3 us
    broadcast_in_dim x3 -> x0, local copies, waits for them, and re-layouts: 4.14 us -> none  [the longest x1 1.8 us: body(): jnp.broadcast_to(packed[top][None], (N_Z, rows, width))]
    unnamed x68 -> x66, local copies, waits for them, and re-layouts: 12.1 us -> 12 us
  transfers between devices with their start and end apart: 35 -> 35, of which waited for: 16 -> 16; matrix products, arithmetic and copies ran while one was open for 15% -> 15% of each run, Pallas kernels for 6% -> 7%
where the time goes in v1:
time: 348 us; the launch traced here: 342 us
  waiting for transfers between devices  167 us (48%)
  starting transfers between devices  70.4 us (20%)
  other arithmetic  30.9 us (9%)
  Pallas kernels  28.5 us (8%)
  local copies, waits for them, and re-layouts  22.3 us (6%)
  matrix products  21.2 us (6%)
    ppermute x9, waiting for transfers between devices, shift_y(): return lax.ppermute(value, 'fsdp', pairs)  85.3 us
    ppermute x15, waiting for transfers between devices, shift_rep(): lax.ppermute(value, 'rep', [(i, (i + step) % N_REP) for i in range(N_REP)])  46.3 us
    all_to_all x5, waiting for transfers between devices, exchange(): lax.all_to_all(value, axis, 0, 0, tiled=True, axis_index_groups=groups)  34.9 us
    all_to_all x5, starting transfers between devices, exchange(): lax.all_to_all(value, axis, 0, 0, tiled=True, axis_index_groups=groups)  33.5 us
    ppermute x15, starting transfers between devices, shift_rep(): lax.ppermute(value, 'rep', [(i, (i + step) % N_REP) for i in range(N_REP)])  17.6 us
    pallas_call x2, Pallas kernels, weight_grads(): pl.pallas_call(kernel, out_shape=[jax.ShapeDtypeStruct((n, 3 * block), dt...  15.6 us
    unnamed x66, local copies, waits for them, and re-layouts  12 us
    ppermute x6, starting transfers between devices, swap_tp(): return lax.ppermute(value, 'tp', [(0, 1), (1, 0)])  10.1 us
  transfers between devices with their start and end apart: 35, of which 16 were waited for; matrix products, arithmetic and copies ran while one was open for 15% of the time, Pallas kernels for 7%

profile of v1, /device:TPU:1, one launch (start us, length us, event | category | flops | bytes accessed | tf_op | source)
XLA Modules:
  0.0 342.1 jit_solution(16339180229821098800)
XLA Ops:
  0.6 2.5 pack.1
  3.2 9.0 %all-to-all-start = ((bf16[8,24,1920]{2,1,0:T(8,128)(2,1)}), bf16[8,24,1920]{2,1,0:T(8,128)(2,1)S(1)}, u32[]{:S(2)}, u32[]{:S(2)}) async-start(bf16[8,24,1920]{2,1,0:T(8,128)(2,1)} %get-tuple-element.32), calls=%async_computation | async-start | bytes 1474560 | tf_op jit(solution)/shard_map/all_to_all | solution.py:39
  13.5 3.0 collective-permute-start.1
  16.9 2.4 collective-permute-start.2
  19.2 9.9 %collective-permute-done.1 = bf16[3,128,768]{2,1,0:T(8,128)(2,1)S(1)} collective-permute-done((bf16[3,128,768]{2,1,0:T(8,128)(2,1)S(1)}, bf16[3,128,768]{2,1,0:T(8,128)(2,1)S(1)}, u32[]{:S(2)}, u32[]{:S(2)}) %collective-permute-start.1) | collective-permute-done | bytes 589856 | tf_op jit(solution)/shard_map/ppermute | solution.py:22
  29.1 13.9 %collective-permute-done = bf16[3,128,768]{2,1,0:T(8,128)(2,1)S(1)} collective-permute-done((bf16[3,128,768]{2,1,0:T(8,128)(2,1)S(1)}, bf16[3,128,768]{2,1,0:T(8,128)(2,1)S(1)}, u32[]{:S(2)}, u32[]{:S(2)}) %collective-permute-start) | collective-permute-done | bytes 589856 | tf_op jit(solution)/shard_map/ppermute | solution.py:22
  43.9 3.0 pad_maximum_fusion
  47.5 2.8 collective-permute-start.6
  52.7 1.8 constant_dynamic-update-slice_fusion
  54.9 1.8 fusion.67
  57.2 24.6 %collective-permute-done.6.refs_3_ = bf16[192,1920]{1,0:T(8,128)(2,1)S(1)} collective-permute-done((bf16[192,1920]{1,0:T(8,128)(2,1)S(1)}, bf16[192,1920]{1,0:T(8,128)(2,1)S(1)}, u32[]{:S(2)}, u32[]{:S(2)}) %collective-permute-start.6) | collective-permute-done | bytes 737312 | tf_op jit(solution)/shard_map/ppermute | solution.py:31
  81.8 4.2 %collective-permute-done.4.refs_1_ = bf16[192,1920]{1,0:T(8,128)(2,1)S(1)} collective-permute-done((bf16[192,1920]{1,0:T(8,128)(2,1)S(1)}, bf16[192,1920]{1,0:T(8,128)(2,1)S(1)}, u32[]{:S(2)}, u32[]{:S(2)}) %collective-permute-start.4) | collective-permute-done | bytes 737312 | tf_op jit(solution)/shard_map/ppermute | solution.py:31
  86.9 3.6 %place.2 = bf16[4,192,1920]{2,1,0:T(8,128)(2,1)} custom-call(s32[1]{0:T(128)} %bitcast.9.me_ref.y_ref, bf16[192,1920]{1,0:T(8,128)(2,1)} %bitcast.139, bf16[192,1920]{1,0:T(8,128)(2,1)} %copy-done.25, bf16[192,1920]{1,0:T(8,128)(2,1)} %copy-done.24, bf16[192,1920]{1,0:T(8,128)(2,1)} %copy-done.22), custom_call_target="tpu_custom_call" | custom-call | flops 1000000 | bytes 5898240 | tf_op jit(solution)/shard_map/place/pallas_call | solution.py:87
  90.5 2.7 fusion.9
  95.9 3.2 multiply_convert_fusion.4
  102.1 1.8 fusion.68
  104.4 6.6 %all-to-all-start.1 = ((bf16[8,24,1920]{2,1,0:T(8,128)(2,1)}), bf16[8,24,1920]{2,1,0:T(8,128)(2,1)}, u32[]{:S(2)}, u32[]{:S(2)}) async-start(bf16[8,24,1920]{2,1,0:T(8,128)(2,1)} %get-tuple-element.40), calls=%async_computation.1 | async-start | bytes 1474560 | tf_op jit(solution)/shard_map/all_to_all | solution.py:39
  111.1 2.1 add.163
  114.3 1.8 collective-permute-start.8
  117.8 15.9 %all-to-all-done.1 = bf16[8,24,1920]{2,1,0:T(8,128)(2,1)} async-done(((bf16[8,24,1920]{2,1,0:T(8,128)(2,1)}), bf16[8,24,1920]{2,1,0:T(8,128)(2,1)}, u32[]{:S(2)}, u32[]{:S(2)}) %all-to-all-start.1) | async-done | bytes 737312 | tf_op jit(solution)/shard_map/all_to_all | solution.py:39
  134.6 2.8 collective-permute-done.9
  139.0 2.1 constant_dynamic-update-slice_fusion.9
  143.5 6.9 %weight_grads.2 = bf16[768,1920]{1,0:T(8,128)(2,1)} custom-call(bf16[1024,768]{1,0:T(8,128)(2,1)S(1)} %multiply_convert_fusion.refs_0_, bf16[1024,768]{1,0:T(8,128)(2,1)} %bitcast.145, bf16[1024,640]{1,0:T(8,128)(2,1)S(1)} %copy-done.2, bf16[1024,640]{1,0:T(8,128)(2,1)S(1)} %get-tuple-element.81.refs_3_, bf16[1024,640]{1,0:T(8,128)(2,1)S(1)} %copy-done, ...), custom_call_target="tpu_custom_call" | custom-call | flops 3019898880 | bytes 10000000 | tf_op jit(solution)/shard_map/weight_grads/pallas_call | solution.py:145
  150.3 4.6 %all-to-all-start.2 = ((bf16[4,192,1920]{2,1,0:T(8,128)(2,1)}), bf16[4,192,1920]{2,1,0:T(8,128)(2,1)}, u32[]{:S(2)}, u32[]{:S(2)}) async-start(bf16[4,192,1920]{2,1,0:T(8,128)(2,1)} %bitcast.140), calls=%async_computation.2 | async-start | bytes 5898240 | tf_op jit(solution)/shard_map/all_to_all | solution.py:39
  156.4 2.2 pad_maximum_fusion.1
  158.6 2.3 collective-permute-start.14
  165.7 38.9 %collective-permute-done.15.refs_1_ = bf16[192,1920]{1,0:T(8,128)(2,1)S(1)} collective-permute-done((bf16[192,1920]{1,0:T(8,128)(2,1)}, bf16[192,1920]{1,0:T(8,128)(2,1)S(1)}, u32[]{:S(2)}, u32[]{:S(2)}) %collective-permute-start.15) | collective-permute-done | bytes 737312 | tf_op jit(solution)/shard_map/ppermute | solution.py:31
  205.5 3.6 %place.3 = bf16[4,192,1920]{2,1,0:T(8,128)(2,1)} custom-call(s32[1]{0:T(128)} %bitcast.9.me_ref.y_ref, bf16[192,1920]{1,0:T(8,128)(2,1)} %bitcast.26.refs_0_, bf16[192,1920]{1,0:T(8,128)(2,1)} %copy-done.23, bf16[192,1920]{1,0:T(8,128)(2,1)} %collective-permute-done.16.refs_2_, bf16[192,1920]{1,0:T(8,128)(2,1)} %collective-permute-done.17.refs_3_), custom_call_target="tpu_custom_call" | custom-call | flops 1000000 | bytes 5898240 | tf_op jit(solution)/shard_map/place/pallas_call | solution.py:87
  217.0 3.1 multiply_convert_fusion.1
  223.3 8.7 %weight_grads.3 = (f32[192,1920]{1,0:T(8,128)}, bf16[192,1920]{1,0:T(8,128)(2,1)S(1)}, bf16[192,1920]{1,0:T(8,128)(2,1)S(1)}, bf16[192,1920]{1,0:T(8,128)(2,1)S(1)}) custom-call(s32[1]{0:T(128)} %bitcast.9.me_ref.y_ref, bf16[1024,768]{1,0:T(8,128)(2,1)} %copy-done.19, bf16[1024,768]{1,0:T(8,128)(2,1)} %bitcast.149, ...), custom_call_target="tpu_custom_call" | custom-call | flops 3019898880 | bytes 10000000 | tf_op jit(solution)/shard_map/weight_grads/pallas_call | solution.py:145
  233.3 2.2 collective-permute-start.18
  235.7 1.8 collective-permute-start.24
  238.4 2.4 convert_reduce_fusion
  242.2 2.5 select_convert_fusion.1
  244.7 6.6 %all-to-all-start.4 = ((f16[8,24,1920]{2,1,0:T(8,128)(2,1)}), f16[8,24,1920]{2,1,0:T(8,128)(2,1)S(1)}, u32[]{:S(2)}, u32[]{:S(2)}) async-start(f16[8,24,1920]{2,1,0:T(8,128)(2,1)} %select_convert_fusion.1), calls=%async_computation.4 | async-start | bytes 1474560 | tf_op jit(solution)/shard_map/all_to_all | solution.py:39
  251.4 2.1 slice_add_fusion
  253.6 17.3 %collective-permute-done.23 = bf16[192,1920]{1,0:T(8,128)(2,1)} collective-permute-done((bf16[192,1920]{1,0:T(8,128)(2,1)S(1)}, bf16[192,1920]{1,0:T(8,128)(2,1)}, u32[]{:S(2)}, u32[]{:S(2)}) %collective-permute-start.23) | collective-permute-done | bytes 737312 | tf_op jit(solution)/shard_map/ppermute | solution.py:31
  271.2 1.8 collective-permute-start.19
  274.8 2.1 abs_reduce_fusion
  276.9 3.0 select_convert_fusion
  280.7 3.1 collective-permute-done.21
  283.8 10.2 %collective-permute-done.20 = f32[128,768]{1,0:T(8,128)S(1)} collective-permute-done((f32[128,768]{1,0:T(8,128)S(1)}, f32[128,768]{1,0:T(8,128)S(1)}, u32[]{:S(2)}, u32[]{:S(2)}) %collective-permute-start.20) | collective-permute-done | bytes 393248 | tf_op jit(solution)/shard_map/ppermute | solution.py:22
  294.2 6.7 %all-to-all-start.3 = ((f16[8,24,1920]{2,1,0:T(8,128)(2,1)}), f16[8,24,1920]{2,1,0:T(8,128)(2,1)S(1)}, u32[]{:S(2)}, u32[]{:S(2)}) async-start(f16[8,24,1920]{2,1,0:T(8,128)(2,1)} %bitcast.41), calls=%async_computation.3 | async-start | bytes 1474560 | tf_op jit(solution)/shard_map/all_to_all | solution.py:39
  304.4 19.0 %all-to-all-done.3 = f16[8,24,1920]{2,1,0:T(8,128)(2,1)S(1)} async-done(((f16[8,24,1920]{2,1,0:T(8,128)(2,1)}), f16[8,24,1920]{2,1,0:T(8,128)(2,1)S(1)}, u32[]{:S(2)}, u32[]{:S(2)}) %all-to-all-start.3) | async-done | bytes 737312 | tf_op jit(solution)/shard_map/all_to_all | solution.py:39
  324.5 2.7 collective-permute-start.28
  327.4 4.0 %collective-permute-done.26 = f16[2,24,1920]{2,1,0:T(8,128)(2,1)S(1)} collective-permute-done((f16[2,24,1920]{2,1,0:T(8,128)(2,1)S(1)}, f16[2,24,1920]{2,1,0:T(8,128)(2,1)S(1)}, u32[]{:S(2)}, u32[]{:S(2)}) %collective-permute-start.26) | collective-permute-done | bytes 184352 | tf_op jit(solution)/shard_map/ppermute | solution.py:22
  334.3 3.8 %collective-permute-start.29 = (f32[2,24]{1,0:T(2,128)S(1)}, f32[2,24]{1,0:T(2,128)S(1)}, u32[]{:S(2)}, u32[]{:S(2)}) collective-permute-start(f32[2,24]{1,0:T(2,128)S(1)} %add_add_fusion.1), channel_id=1, source_target_pairs={{0,1},{1,0},{2,3},{3,2},{4,5},{5,4},{6,7},{7,6},{8,9},{9,8},{10,11... | collective-permute-start | bytes 584 | tf_op jit(solution)/shard_map/ppermute | solution.py:26
  338.1 3.2 finish.1
  (178 shorter events, 54.4 us)
Async XLA Ops:
  0.6 11.5 %copy-start.26 = (bf16[2,256,768]{2,1,0:T(8,128)(2,1)S(1)}, bf16[2,256,768]{2,1,0:T(8,128)(2,1)}, u32[]{:S(2)}) copy-start(bf16[2,256,768]{2,1,0:T(8,128)(2,1)} %param.10) | copy-start | bytes 2359300
  3.2 40.7 %all-to-all-start = ((bf16[8,24,1920]{2,1,0:T(8,128)(2,1)}), bf16[8,24,1920]{2,1,0:T(8,128)(2,1)S(1)}, u32[]{:S(2)}, u32[]{:S(2)}) async-start(bf16[8,24,1920]{2,1,0:T(8,128)(2,1)} %get-tuple-element.32), calls=%async_computation | async-start | bytes 1474560 | tf_op jit(solution)/shard_map/all_to_all | solution.py:39
  12.3 35.1 %copy-start.12 = (bf16[1,128,768]{2,1,0:T(8,128)(2,1)}, bf16[1,128,768]{2,1,0:T(8,128)(2,1)S(1)}, u32[]{:S(2)}) copy-start(bf16[1,128,768]{2,1,0:T(8,128)(2,1)S(1)} %get-tuple-element.95) | copy-start | bytes 589828
  13.5 15.6 %collective-permute-start.1 = (bf16[3,128,768]{2,1,0:T(8,128)(2,1)S(1)}, bf16[3,128,768]{2,1,0:T(8,128)(2,1)S(1)}, u32[]{:S(2)}, u32[]{:S(2)}) collective-permute-start(bf16[3,128,768]{2,1,0:T(8,128)(2,1)S(1)} %get-tuple-element.97), channel_id=1, source_target_pairs={{0,128},{64,192},{128,0},{192,64},{1,129},{65,193},{129,1},{193,65... | collective-permute-start | bytes 1769480 | tf_op jit(solution)/shard_map/ppermute | solution.py:22
  16.6 26.5 %collective-permute-start = (bf16[3,128,768]{2,1,0:T(8,128)(2,1)S(1)}, bf16[3,128,768]{2,1,0:T(8,128)(2,1)S(1)}, u32[]{:S(2)}, u32[]{:S(2)}) collective-permute-start(bf16[3,128,768]{2,1,0:T(8,128)(2,1)S(1)} %get-tuple-element.97), channel_id=1, source_target_pairs={{0,64},{64,128},{128,192},{192,0},{1,65},{65,129},{129,193},{193,1... | collective-permute-start | bytes 1769480 | tf_op jit(solution)/shard_map/ppermute | solution.py:22
  16.9 27.0 %collective-permute-start.2 = (bf16[3,128,768]{2,1,0:T(8,128)(2,1)S(1)}, bf16[3,128,768]{2,1,0:T(8,128)(2,1)S(1)}, u32[]{:S(2)}, u32[]{:S(2)}) collective-permute-start(bf16[3,128,768]{2,1,0:T(8,128)(2,1)S(1)} %get-tuple-element.97), channel_id=1, source_target_pairs={{0,192},{64,0},{128,64},{192,128},{1,193},{65,1},{129,65},{193,129... | collective-permute-start | bytes 1769480 | tf_op jit(solution)/shard_map/ppermute | solution.py:22
  43.9 6.8 %copy-start.13 = (bf16[8,24,1920]{2,1,0:T(8,128)(2,1)}, bf16[8,24,1920]{2,1,0:T(8,128)(2,1)S(1)}, u32[]{:S(2)}) copy-start(bf16[8,24,1920]{2,1,0:T(8,128)(2,1)S(1)} %all-to-all-done) | copy-start | bytes 2211844
  46.9 5.8 %collective-permute-start.3 = (bf16[4,3,128,768]{3,2,1,0:T(8,128)(2,1)}, bf16[4,3,128,768]{3,2,1,0:T(8,128)(2,1)}, u32[]{:S(2)}, u32[]{:S(2)}) collective-permute-start(bf16[4,3,128,768]{3,2,1,0:T(8,128)(2,1)} %pad_maximum_fusion), channel_id=1, source_target_pairs={{0,1},{1,0},{2,3},{3,2},{4,5},{5,4},{6,7},{7,6},{8,9},{9,8},{10,11... | collective-permute-start | bytes 7077896 | tf_op jit(solution)/shard_map/ppermute | solution.py:26
  47.5 34.3 %collective-permute-start.6 = (bf16[192,1920]{1,0:T(8,128)(2,1)S(1)}, bf16[192,1920]{1,0:T(8,128)(2,1)S(1)}, u32[]{:S(2)}, u32[]{:S(2)}) collective-permute-start(bf16[192,1920]{1,0:T(8,128)(2,1)S(1)} %bitcast.136), channel_id=1, source_target_pairs={{0,48},{2,50},{4,52},{6,54},{8,56},{10,58},{12,60},{14,62},{16,0},... | collective-permute-start | bytes 2211848 | tf_op jit(solution)/shard_map/ppermute | solution.py:31
  50.3 31.5 %collective-permute-start.5 = (bf16[192,1920]{1,0:T(8,128)(2,1)S(1)}, bf16[192,1920]{1,0:T(8,128)(2,1)S(1)}, u32[]{:S(2)}, u32[]{:S(2)}) collective-permute-start(bf16[192,1920]{1,0:T(8,128)(2,1)S(1)} %bitcast.137), channel_id=1, source_target_pairs={{0,32},{2,34},{4,36},{6,38},{8,40},{10,42},{12,44},{14,46},{16,48}... | collective-permute-start | bytes 2211848 | tf_op jit(solution)/shard_map/ppermute | solution.py:31
  50.6 35.4 %collective-permute-start.4 = (bf16[192,1920]{1,0:T(8,128)(2,1)S(1)}, bf16[192,1920]{1,0:T(8,128)(2,1)S(1)}, u32[]{:S(2)}, u32[]{:S(2)}) collective-permute-start(bf16[192,1920]{1,0:T(8,128)(2,1)S(1)} %bitcast.138), channel_id=1, source_target_pairs={{0,16},{2,18},{4,20},{6,22},{8,24},{10,26},{12,28},{14,30},{16,32}... | collective-permute-start | bytes 2211848 | tf_op jit(solution)/shard_map/ppermute | solution.py:31
  57.2 33.3 %copy-start.21 = (bf16[8,1,128,768]{3,2,1,0:T(8,128)(2,1)}, bf16[8,1,128,768]{3,2,1,0:T(8,128)(2,1)S(1)}, u32[]{:S(2)}) copy-start(bf16[8,1,128,768]{3,2,1,0:T(8,128)(2,1)S(1)} %get-tuple-element.83) | copy-start | bytes 4718596
  103.9 7.2 %collective-permute-start.7 = (f32[4,128,768]{2,1,0:T(8,128)}, f32[4,128,768]{2,1,0:T(8,128)}, u32[]{:S(2)}, u32[]{:S(2)}) collective-permute-start(f32[4,128,768]{2,1,0:T(8,128)} %bitcast.14), channel_id=1, source_target_pairs={{0,1},{1,0},{2,3},{3,2},{4,5},{5,4},{6,7},{7,6},{8,9},{9,8},{10,11... | collective-permute-start | bytes 4718600 | tf_op jit(solution)/shard_map/ppermute | solution.py:26
  104.4 29.3 %all-to-all-start.1 = ((bf16[8,24,1920]{2,1,0:T(8,128)(2,1)}), bf16[8,24,1920]{2,1,0:T(8,128)(2,1)}, u32[]{:S(2)}, u32[]{:S(2)}) async-start(bf16[8,24,1920]{2,1,0:T(8,128)(2,1)} %get-tuple-element.40), calls=%async_computation.1 | async-start | bytes 1474560 | tf_op jit(solution)/shard_map/all_to_all | solution.py:39
  114.3 20.3 %collective-permute-start.8 = (f32[128,768]{1,0:T(8,128)}, f32[128,768]{1,0:T(8,128)}, u32[]{:S(2)}, u32[]{:S(2)}) collective-permute-start(f32[128,768]{1,0:T(8,128)} %get-tuple-element.89), channel_id=1, source_target_pairs={{0,192},{64,0},{128,64},{192,128},{1,193},{65,1},{129,65},{193,129... | collective-permute-start | bytes 1179656 | tf_op jit(solution)/shard_map/ppermute | solution.py:22
  116.1 18.5 %collective-permute-start.10 = (f32[128,768]{1,0:T(8,128)}, f32[128,768]{1,0:T(8,128)}, u32[]{:S(2)}, u32[]{:S(2)}) collective-permute-start(f32[128,768]{1,0:T(8,128)} %get-tuple-element.90), channel_id=1, source_target_pairs={{0,128},{64,192},{128,0},{192,64},{1,129},{65,193},{129,1},{193,65... | collective-permute-start | bytes 1179656 | tf_op jit(solution)/shard_map/ppermute | solution.py:22
  117.5 19.8 %collective-permute-start.9 = (f32[128,768]{1,0:T(8,128)}, f32[128,768]{1,0:T(8,128)}, u32[]{:S(2)}, u32[]{:S(2)}) collective-permute-start(f32[128,768]{1,0:T(8,128)} %get-tuple-element.91), channel_id=1, source_target_pairs={{0,64},{64,128},{128,192},{192,0},{1,65},{65,129},{129,193},{193,1... | collective-permute-start | bytes 1179656 | tf_op jit(solution)/shard_map/ppermute | solution.py:22
  133.7 9.8 %copy-start = (bf16[1024,640]{1,0:T(8,128)(2,1)S(1)}, bf16[1024,640]{1,0:T(8,128)(2,1)}, u32[]{:S(2)}) copy-start(bf16[1024,640]{1,0:T(8,128)(2,1)} %get-tuple-element.79.refs_4_) | copy-start | bytes 3932164
  133.7 9.8 %copy-start.2 = (bf16[1024,640]{1,0:T(8,128)(2,1)S(1)}, bf16[1024,640]{1,0:T(8,128)(2,1)}, u32[]{:S(2)}) copy-start(bf16[1024,640]{1,0:T(8,128)(2,1)} %copy-done.1) | copy-start | bytes 3932164
  133.7 32.0 %collective-permute-start.17 = (bf16[192,1920]{1,0:T(8,128)(2,1)}, bf16[192,1920]{1,0:T(8,128)(2,1)}, u32[]{:S(2)}, u32[]{:S(2)}) collective-permute-start(bf16[192,1920]{1,0:T(8,128)(2,1)} %bitcast.26.refs_0_), channel_id=1, source_target_pairs={{0,48},{2,50},{4,52},{6,54},{8,56},{10,58},{12,60},{14,62},{16,0},... | collective-permute-start | bytes 2211848 | tf_op jit(solution)/shard_map/ppermute | solution.py:31
  134.3 31.4 %collective-permute-start.16 = (bf16[192,1920]{1,0:T(8,128)(2,1)}, bf16[192,1920]{1,0:T(8,128)(2,1)}, u32[]{:S(2)}, u32[]{:S(2)}) collective-permute-start(bf16[192,1920]{1,0:T(8,128)(2,1)} %bitcast.26.refs_0_), channel_id=1, source_target_pairs={{0,32},{2,34},{4,36},{6,38},{8,40},{10,42},{12,44},{14,46},{16,48}... | collective-permute-start | bytes 2211848 | tf_op jit(solution)/shard_map/ppermute | solution.py:31
  141.2 13.8 %collective-permute-start.13 = (bf16[128,768]{1,0:T(8,128)(2,1)}, bf16[128,768]{1,0:T(8,128)(2,1)}, u32[]{:S(2)}, u32[]{:S(2)}) collective-permute-start(bf16[128,768]{1,0:T(8,128)(2,1)} %get-tuple-element.70), channel_id=1, source_target_pairs={{0,192},{64,0},{128,64},{192,128},{1,193},{65,1},{129,65},{193,129... | collective-permute-start | bytes 589832 | tf_op jit(solution)/shard_map/ppermute | solution.py:22
  141.2 15.2 %collective-permute-start.12 = (bf16[128,768]{1,0:T(8,128)(2,1)}, bf16[128,768]{1,0:T(8,128)(2,1)}, u32[]{:S(2)}, u32[]{:S(2)}) collective-permute-start(bf16[128,768]{1,0:T(8,128)(2,1)} %get-tuple-element.70), channel_id=1, source_target_pairs={{0,128},{64,192},{128,0},{192,64},{1,129},{65,193},{129,1},{193,65... | collective-permute-start | bytes 589832 | tf_op jit(solution)/shard_map/ppermute | solution.py:22
  142.6 13.8 %collective-permute-start.11 = (bf16[128,768]{1,0:T(8,128)(2,1)}, bf16[128,768]{1,0:T(8,128)(2,1)}, u32[]{:S(2)}, u32[]{:S(2)}) collective-permute-start(bf16[128,768]{1,0:T(8,128)(2,1)} %get-tuple-element.70), channel_id=1, source_target_pairs={{0,64},{64,128},{128,192},{192,0},{1,65},{65,129},{129,193},{193,1... | collective-permute-start | bytes 589832 | tf_op jit(solution)/shard_map/ppermute | solution.py:22
  150.3 88.1 %all-to-all-start.2 = ((bf16[4,192,1920]{2,1,0:T(8,128)(2,1)}), bf16[4,192,1920]{2,1,0:T(8,128)(2,1)}, u32[]{:S(2)}, u32[]{:S(2)}) async-start(bf16[4,192,1920]{2,1,0:T(8,128)(2,1)} %bitcast.140), calls=%async_computation.2 | async-start | bytes 5898240 | tf_op jit(solution)/shard_map/all_to_all | solution.py:39
  154.9 49.7 %copy-start.3 = (bf16[8,1,128,768]{3,2,1,0:T(8,128)(2,1)S(1)}, bf16[8,1,128,768]{3,2,1,0:T(8,128)(2,1)}, u32[]{:S(2)}) copy-start(bf16[8,1,128,768]{3,2,1,0:T(8,128)(2,1)} %get-tuple-element.82) | copy-start | bytes 4718596
  155.0 49.7 %collective-permute-start.15 = (bf16[192,1920]{1,0:T(8,128)(2,1)}, bf16[192,1920]{1,0:T(8,128)(2,1)S(1)}, u32[]{:S(2)}, u32[]{:S(2)}) collective-permute-start(bf16[192,1920]{1,0:T(8,128)(2,1)} %bitcast.26.refs_0_), channel_id=1, source_target_pairs={{0,16},{2,18},{4,20},{6,22},{8,24},{10,26},{12,28},{14,30},{16,32}... | collective-permute-start | bytes 2211848 | tf_op jit(solution)/shard_map/ppermute | solution.py:31
  158.6 54.1 %collective-permute-start.14 = (bf16[4,128,768]{2,1,0:T(8,128)(2,1)}, bf16[4,128,768]{2,1,0:T(8,128)(2,1)}, u32[]{:S(2)}, u32[]{:S(2)}) collective-permute-start(bf16[4,128,768]{2,1,0:T(8,128)(2,1)} %pad_maximum_fusion.1), channel_id=1, source_target_pairs={{0,1},{1,0},{2,3},{3,2},{4,5},{5,4},{6,7},{7,6},{8,9},{9,8},{10,11... | collective-permute-start | bytes 2359304 | tf_op jit(solution)/shard_map/ppermute | solution.py:26
  223.0 9.0 %copy-start.7 = (f32[1024,768]{1,0:T(8,128)}, f32[1024,768]{1,0:T(8,128)S(1)}, u32[]{:S(2)}) copy-start(f32[1024,768]{1,0:T(8,128)S(1)} %get-tuple-element.107) | copy-start | bytes 9437188
  233.3 18.1 %collective-permute-start.18 = (f32[4,128,768]{2,1,0:T(8,128)}, f32[4,128,768]{2,1,0:T(8,128)}, u32[]{:S(2)}, u32[]{:S(2)}) collective-permute-start(f32[4,128,768]{2,1,0:T(8,128)} %slice.139), channel_id=1, source_target_pairs={{0,1},{1,0},{2,3},{3,2},{4,5},{5,4},{6,7},{7,6},{8,9},{9,8},{10,11... | collective-permute-start | bytes 4718600 | tf_op jit(solution)/shard_map/ppermute | solution.py:26
  235.5 35.3 %collective-permute-start.23 = (bf16[192,1920]{1,0:T(8,128)(2,1)S(1)}, bf16[192,1920]{1,0:T(8,128)(2,1)}, u32[]{:S(2)}, u32[]{:S(2)}) collective-permute-start(bf16[192,1920]{1,0:T(8,128)(2,1)S(1)} %get-tuple-element.48), channel_id=1, source_target_pairs={{0,16},{2,18},{4,20},{6,22},{8,24},{10,26},{12,28},{14,30},{16,32}... | collective-permute-start | bytes 2211848 | tf_op jit(solution)/shard_map/ppermute | solution.py:31
  235.7 35.1 %collective-permute-start.24 = (bf16[192,1920]{1,0:T(8,128)(2,1)S(1)}, bf16[192,1920]{1,0:T(8,128)(2,1)}, u32[]{:S(2)}, u32[]{:S(2)}) collective-permute-start(bf16[192,1920]{1,0:T(8,128)(2,1)S(1)} %get-tuple-element.49), channel_id=1, source_target_pairs={{0,32},{2,34},{4,36},{6,38},{8,40},{10,42},{12,44},{14,46},{16,48}... | collective-permute-start | bytes 2211848 | tf_op jit(solution)/shard_map/ppermute | solution.py:31
  237.5 33.7 %collective-permute-start.25 = (bf16[192,1920]{1,0:T(8,128)(2,1)S(1)}, bf16[192,1920]{1,0:T(8,128)(2,1)}, u32[]{:S(2)}, u32[]{:S(2)}) collective-permute-start(bf16[192,1920]{1,0:T(8,128)(2,1)S(1)} %get-tuple-element.50), channel_id=1, source_target_pairs={{0,48},{2,50},{4,52},{6,54},{8,56},{10,58},{12,60},{14,62},{16,0},... | collective-permute-start | bytes 2211848 | tf_op jit(solution)/shard_map/ppermute | solution.py:31
  244.7 49.5 %all-to-all-start.4 = ((f16[8,24,1920]{2,1,0:T(8,128)(2,1)}), f16[8,24,1920]{2,1,0:T(8,128)(2,1)S(1)}, u32[]{:S(2)}, u32[]{:S(2)}) async-start(f16[8,24,1920]{2,1,0:T(8,128)(2,1)} %select_convert_fusion.1), calls=%async_computation.4 | async-start | bytes 1474560 | tf_op jit(solution)/shard_map/all_to_all | solution.py:39
  253.5 21.4 %copy-start.11 = (f32[192,1920]{1,0:T(8,128)S(1)}, f32[192,1920]{1,0:T(8,128)}, u32[]{:S(2)}) copy-start(f32[192,1920]{1,0:T(8,128)} %get-tuple-element.47) | copy-start | bytes 4423684
  271.2 9.5 %collective-permute-start.19 = (f32[128,768]{1,0:T(8,128)S(1)}, f32[128,768]{1,0:T(8,128)S(1)}, u32[]{:S(2)}, u32[]{:S(2)}) collective-permute-start(f32[128,768]{1,0:T(8,128)S(1)} %get-tuple-element.86), channel_id=1, source_target_pairs={{0,192},{64,0},{128,64},{192,128},{1,193},{65,1},{129,65},{193,129... | collective-permute-start | bytes 1179656 | tf_op jit(solution)/shard_map/ppermute | solution.py:22
  273.0 10.8 %collective-permute-start.21 = (f32[128,768]{1,0:T(8,128)S(1)}, f32[128,768]{1,0:T(8,128)S(1)}, u32[]{:S(2)}, u32[]{:S(2)}) collective-permute-start(f32[128,768]{1,0:T(8,128)S(1)} %get-tuple-element.87), channel_id=1, source_target_pairs={{0,128},{64,192},{128,0},{192,64},{1,129},{65,193},{129,1},{193,65... | collective-permute-start | bytes 1179656 | tf_op jit(solution)/shard_map/ppermute | solution.py:22
  274.0 20.0 %collective-permute-start.20 = (f32[128,768]{1,0:T(8,128)S(1)}, f32[128,768]{1,0:T(8,128)S(1)}, u32[]{:S(2)}, u32[]{:S(2)}) collective-permute-start(f32[128,768]{1,0:T(8,128)S(1)} %get-tuple-element.88), channel_id=1, source_target_pairs={{0,64},{64,128},{128,192},{192,0},{1,65},{65,129},{129,193},{193,1... | collective-permute-start | bytes 1179656 | tf_op jit(solution)/shard_map/ppermute | solution.py:22
  279.8 21.1 %copy-start.20 = (f32[128,768]{1,0:T(8,128)S(1)}, f32[128,768]{1,0:T(8,128)}, u32[]{:S(2)}) copy-start(f32[128,768]{1,0:T(8,128)} %get-tuple-element.71) | copy-start | bytes 1179652
  294.2 29.2 %all-to-all-start.3 = ((f16[8,24,1920]{2,1,0:T(8,128)(2,1)}), f16[8,24,1920]{2,1,0:T(8,128)(2,1)S(1)}, u32[]{:S(2)}, u32[]{:S(2)}) async-start(f16[8,24,1920]{2,1,0:T(8,128)(2,1)} %bitcast.41), calls=%async_computation.3 | async-start | bytes 1474560 | tf_op jit(solution)/shard_map/all_to_all | solution.py:39
  301.1 2.2 collective-permute-start.22
  324.4 7.0 %collective-permute-start.26 = (f16[2,24,1920]{2,1,0:T(8,128)(2,1)S(1)}, f16[2,24,1920]{2,1,0:T(8,128)(2,1)S(1)}, u32[]{:S(2)}, u32[]{:S(2)}) collective-permute-start(f16[2,24,1920]{2,1,0:T(8,128)(2,1)S(1)} %pad_maximum_fusion.4), channel_id=1, source_target_pairs={{0,64},{64,128},{128,192},{192,0},{1,65},{65,129},{129,193},{193,1... | collective-permute-start | bytes 552968 | tf_op jit(solution)/shard_map/ppermute | solution.py:22
  324.5 7.2 %collective-permute-start.28 = (f16[2,24,1920]{2,1,0:T(8,128)(2,1)S(1)}, f16[2,24,1920]{2,1,0:T(8,128)(2,1)S(1)}, u32[]{:S(2)}, u32[]{:S(2)}) collective-permute-start(f16[2,24,1920]{2,1,0:T(8,128)(2,1)S(1)} %pad_maximum_fusion.4), channel_id=1, source_target_pairs={{0,192},{64,0},{128,64},{192,128},{1,193},{65,1},{129,65},{193,129... | collective-permute-start | bytes 552968 | tf_op jit(solution)/shard_map/ppermute | solution.py:22
  327.1 6.7 %collective-permute-start.27 = (f16[2,24,1920]{2,1,0:T(8,128)(2,1)S(1)}, f16[2,24,1920]{2,1,0:T(8,128)(2,1)S(1)}, u32[]{:S(2)}, u32[]{:S(2)}) collective-permute-start(f16[2,24,1920]{2,1,0:T(8,128)(2,1)S(1)} %pad_maximum_fusion.4), channel_id=1, source_target_pairs={{0,128},{64,192},{128,0},{192,64},{1,129},{65,193},{129,1},{193,65... | collective-permute-start | bytes 552968 | tf_op jit(solution)/shard_map/ppermute | solution.py:22
  327.2 10.9 %copy-start.15 = (f32[2,24,1920]{2,1,0:T(8,128)}, f32[2,24,1920]{2,1,0:T(8,128)S(1)}, u32[]{:S(2)}) copy-start(f32[2,24,1920]{2,1,0:T(8,128)S(1)} %convert_multiply_fusion.9.b0) | copy-start | bytes 1105924
  327.3 14.1 %copy-start.29 = (f32[2,24]{1,0:T(2,128)S(1)}, f32[2,24]{1,0:T(2,128)}, u32[]{:S(2)}) copy-start(f32[2,24]{1,0:T(2,128)} %param.19) | copy-start | bytes 580
  331.7 6.5 %copy-start.16 = (f32[2,24,1920]{2,1,0:T(8,128)}, f32[2,24,1920]{2,1,0:T(8,128)S(1)}, u32[]{:S(2)}) copy-start(f32[2,24,1920]{2,1,0:T(8,128)S(1)} %convert_multiply_fusion.8.b1) | copy-start | bytes 1105924
  334.3 7.0 %collective-permute-start.29 = (f32[2,24]{1,0:T(2,128)S(1)}, f32[2,24]{1,0:T(2,128)S(1)}, u32[]{:S(2)}, u32[]{:S(2)}) collective-permute-start(f32[2,24]{1,0:T(2,128)S(1)} %add_add_fusion.1), channel_id=1, source_target_pairs={{0,1},{1,0},{2,3},{3,2},{4,5},{5,4},{6,7},{7,6},{8,9},{9,8},{10,11... | collective-permute-start | bytes 584 | tf_op jit(solution)/shard_map/ppermute | solution.py:26
  (17 other events, 48.1 us)
